TPU v7x, 32 devices: a 4x2x2 block of a 4x4x8 slice. The times are simulated.
32 devices in a mesh: seqs: 4 (over y, z), states: 8 (over x, core).
Axes of the slice: x: 4, y: 2, z: 2, core: 2. Of those that a mesh axis runs over, the one named last changes fastest.
The devices are a block of a 4x4x8 slice.
Arguments:
- trans_mat: bfloat16 [16384, 16384], P(None, 'states')
- emit_mat: bfloat16 [16384, 10000], P('states')
- init_prob: float32 [16384], P('states')
- tokens: int32 [512, 8], P('seqs'), parts along dimension 0
- lengths: int32 [512], P('seqs'), parts along dimension 0
Outputs:
- output 1: float32 [512], P('seqs'), parts along dimension 0
- output 2: float32 [512, 16384], P('seqs', 'states'), parts along dimension 0
- output 3: float32 [65536, 2048], P(('seqs', 'states')), parts along dimension 0
There are 4 independent parts. A program takes and returns all parts, laid end to end along the dimension named above; an argument that names none is the same for every part.
All inputs are finite; a program needn't handle non-finite values.
Results may differ from a plain program's by a relative error of at most 0.001.
Values are sent between devices in bfloat16 or wider.
A program may use at most 768 MiB of HBM per device.

v0:
```python
import jax
import jax.numpy as jnp
from jax import lax
from jax.sharding import PartitionSpec as P


def solution(mesh):
    def step_weight(live_mask, emit_now, beta_cur, step_scale):
        scaled = emit_now.astype(jnp.float32) * beta_cur / step_scale[:, None]
        return jnp.where(live_mask[:, None], scaled, 0.0).astype(jnp.bfloat16)

    def local_run(trans_loc, emit_loc, init_loc, tokens_loc, lengths_loc):
        seq_count, step_count = tokens_loc.shape
        block_size = trans_loc.shape[1]
        group_idx = lax.axis_index('states')
        emit_seq = jnp.transpose(jnp.take(emit_loc, tokens_loc.T, axis=1), (1, 2, 0))
        first_mass = init_loc[None, :] * emit_seq[0].astype(jnp.float32)
        first_norm = lax.psum(jnp.sum(first_mass, axis=1), 'states')
        alpha_first = first_mass / first_norm[:, None]
        live_steps = jnp.arange(1, step_count)[:, None] < lengths_loc[None, :]

        def forward_step(alpha_cur, inputs):
            live_mask, emit_now = inputs
            alpha_bf = alpha_cur.astype(jnp.bfloat16)
            alpha_full = lax.all_gather(alpha_bf, 'states', axis=1, tiled=True)
            pred_mass = jnp.dot(alpha_full, trans_loc, preferred_element_type=jnp.float32)
            new_mass = pred_mass * emit_now.astype(jnp.float32)
            norm_sum = lax.psum(jnp.sum(new_mass, axis=1), 'states')
            step_scale = jnp.where(live_mask, norm_sum, 1.0)
            alpha_next = jnp.where(live_mask[:, None], new_mass / norm_sum[:, None], alpha_cur)
            return alpha_next, (alpha_bf, step_scale)

        alpha_last, (alpha_prev, scales) = lax.scan(forward_step, alpha_first, (live_steps, emit_seq[1:]))
        loglik = jnp.log(first_norm) + jnp.sum(jnp.log(scales), axis=0)

        def backward_step(beta_cur, inputs):
            live_mask, emit_now, step_scale = inputs
            weight = step_weight(live_mask, emit_now, beta_cur, step_scale)
            partial_sum = lax.dot_general(weight, trans_loc, (((1,), (1,)), ((), ())), preferred_element_type=jnp.float32)
            beta_prev = lax.psum_scatter(partial_sum, 'states', scatter_dimension=1, tiled=True)
            return beta_prev + jnp.where(live_mask, 0.0, 1.0)[:, None], weight

        beta_one, late_weights = lax.scan(backward_step, jnp.ones((seq_count, block_size), jnp.float32), (live_steps[1:], emit_seq[2:], scales[1:]), reverse=True)
        first_weight = step_weight(live_steps[0], emit_seq[1], beta_one, scales[0])
        pair_sum = jnp.einsum('tbi,tbj->ij', alpha_prev[1:], late_weights, preferred_element_type=jnp.float32)
        pair_sum = pair_sum + lax.dot_general(alpha_prev[0], first_weight, (((0,), (0,)), ((), ())), preferred_element_type=jnp.float32)
        diag_block = lax.dynamic_slice_in_dim(trans_loc, group_idx * block_size, block_size, axis=0)
        counts = diag_block.astype(jnp.float32) * pair_sum
        return loglik, alpha_last, counts

    return jax.shard_map(local_run, mesh=mesh, in_specs=(P(None, 'states'), P('states', None), P('states'), P('seqs', None), P('seqs')), out_specs=(P('seqs'), P('seqs', 'states'), P(('seqs', 'states'), None)), check_vma=False)
```

profile of v0, /device:TPU:81, one launch (start us, length us, event | category | flops | bytes accessed | tf_op | source)
XLA Modules:
  0.0 1074.8 jit_solution(1110485615016695043)
XLA Ops:
  10.5 24.2 %gather_fusion = bf16[1024,2048]{1,0:T(8,128)(2,1)} fusion(bf16[2048,10000]{0,1:T(8,128)(2,1)} %param.10, s32[1024]{0:T(1024)S(1)} %bitcast_clamp_fusion), kind=kCustom, calls=%fused_computation | custom fusion | bytes 8392704 | tf_op jit(solution)/shard_map/jit(_take)/gather | solution.py:16
  39.5 14.0 %psum.14 = f32[128]{0:T(128)S(1)} all-reduce(f32[128]{0:T(128)S(1)} %fusion.11), channel_id=1, replica_groups=mesh['seqs'=4,'states'=8] {'states'}, use_global_device_ids=true, to_apply=%region_1.2 | all-reduce | flops 128 | bytes 1024 | tf_op jit(solution)/shard_map/psum | solution.py:18
  61.3 485.7 %while.31 = (s32[]{:T(128)}, f32[128,2048]{1,0:T(8,128)S(1)}, bf16[7,128,2048]{2,1,0:T(8,128)(2,1)}, f32[7,128]{1,0:T(8,128)S(1)}, pred[7,128]{1,0:T(8,128)(4,1)...) while((s32[]{:T(128)}, f32[128,2048]{1,0:T(8,128)S(1)}, ...), condition=%wide.region_5.6_spmd, body=%wide.region_2.0_spmd.sunk | while | flops 8591507456 | bytes 92279312 | solution.py:33
  62.5 33.6 %all-gather.2.cloned.1.call-done = bf16[128,16384]{1,0:T(8,128)(2,1)} async-done(((bf16[128,2048]{1,0:T(8,128)(2,1)}), bf16[128,16384]{1,0:T(8,128)(2,1)}) %all-gather.2.cloned.1.call-update) | async-done | bytes 4194320 | tf_op jit(solution)/shard_map/while/body/eval_jaxpr/all_gather | solution.py:25
  96.1 25.1 %fusion.35 = (f32[128]{0:T(128)S(1)}, f32[128,2048]{1,0:T(8,128)S(1)}) fusion(bf16[7,128,2048]{2,1,0:T(8,128)(2,1)} %get-tuple-element.375, s32[]{:T(128)S(6)} %copy.16, bf16[128,16384]{1,0:T(8,128)(2,1)} %all-gather.2.cloned.1.call-done, bf16[16384,2048]{1,0:T(8,128)(2,1)} %get-tuple-element.374), kind=kOutput, calls=%fused_computation.44.clone.1 | convolution fusion | flops 8590721024 | bytes 72876544 | tf_op jit(solution)/shard_map/while/body/eval_jaxpr/dot_general | solution.py:26
  134.9 30.3 %all-gather.2.cloned.1.call-done = bf16[128,16384]{1,0:T(8,128)(2,1)} async-done(((bf16[128,2048]{1,0:T(8,128)(2,1)}), bf16[128,16384]{1,0:T(8,128)(2,1)}) %all-gather.2.cloned.1.call-update) | async-done | bytes 4194320 | tf_op jit(solution)/shard_map/while/body/eval_jaxpr/all_gather | solution.py:25
  165.2 25.1 %fusion.35 = (f32[128]{0:T(128)S(1)}, f32[128,2048]{1,0:T(8,128)S(1)}) fusion(bf16[7,128,2048]{2,1,0:T(8,128)(2,1)} %get-tuple-element.375, s32[]{:T(128)S(6)} %copy.16, bf16[128,16384]{1,0:T(8,128)(2,1)} %all-gather.2.cloned.1.call-done, bf16[16384,2048]{1,0:T(8,128)(2,1)} %get-tuple-element.374), kind=kOutput, calls=%fused_computation.44.clone.1 | convolution fusion | flops 8590721024 | bytes 72876544 | tf_op jit(solution)/shard_map/while/body/eval_jaxpr/dot_general | solution.py:26
  203.9 30.4 %all-gather.2.cloned.1.call-done = bf16[128,16384]{1,0:T(8,128)(2,1)} async-done(((bf16[128,2048]{1,0:T(8,128)(2,1)}), bf16[128,16384]{1,0:T(8,128)(2,1)}) %all-gather.2.cloned.1.call-update) | async-done | bytes 4194320 | tf_op jit(solution)/shard_map/while/body/eval_jaxpr/all_gather | solution.py:25
  234.2 25.1 %fusion.35 = (f32[128]{0:T(128)S(1)}, f32[128,2048]{1,0:T(8,128)S(1)}) fusion(bf16[7,128,2048]{2,1,0:T(8,128)(2,1)} %get-tuple-element.375, s32[]{:T(128)S(6)} %copy.16, bf16[128,16384]{1,0:T(8,128)(2,1)} %all-gather.2.cloned.1.call-done, bf16[16384,2048]{1,0:T(8,128)(2,1)} %get-tuple-element.374), kind=kOutput, calls=%fused_computation.44.clone.1 | convolution fusion | flops 8590721024 | bytes 72876544 | tf_op jit(solution)/shard_map/while/body/eval_jaxpr/dot_general | solution.py:26
  272.9 30.1 %all-gather.2.cloned.1.call-done = bf16[128,16384]{1,0:T(8,128)(2,1)} async-done(((bf16[128,2048]{1,0:T(8,128)(2,1)}), bf16[128,16384]{1,0:T(8,128)(2,1)}) %all-gather.2.cloned.1.call-update) | async-done | bytes 4194320 | tf_op jit(solution)/shard_map/while/body/eval_jaxpr/all_gather | solution.py:25
  303.0 25.1 %fusion.35 = (f32[128]{0:T(128)S(1)}, f32[128,2048]{1,0:T(8,128)S(1)}) fusion(bf16[7,128,2048]{2,1,0:T(8,128)(2,1)} %get-tuple-element.375, s32[]{:T(128)S(6)} %copy.16, bf16[128,16384]{1,0:T(8,128)(2,1)} %all-gather.2.cloned.1.call-done, bf16[16384,2048]{1,0:T(8,128)(2,1)} %get-tuple-element.374), kind=kOutput, calls=%fused_computation.44.clone.1 | convolution fusion | flops 8590721024 | bytes 72876544 | tf_op jit(solution)/shard_map/while/body/eval_jaxpr/dot_general | solution.py:26
  341.7 30.0 %all-gather.2.cloned.1.call-done = bf16[128,16384]{1,0:T(8,128)(2,1)} async-done(((bf16[128,2048]{1,0:T(8,128)(2,1)}), bf16[128,16384]{1,0:T(8,128)(2,1)}) %all-gather.2.cloned.1.call-update) | async-done | bytes 4194320 | tf_op jit(solution)/shard_map/while/body/eval_jaxpr/all_gather | solution.py:25
  371.7 25.1 %fusion.35 = (f32[128]{0:T(128)S(1)}, f32[128,2048]{1,0:T(8,128)S(1)}) fusion(bf16[7,128,2048]{2,1,0:T(8,128)(2,1)} %get-tuple-element.375, s32[]{:T(128)S(6)} %copy.16, bf16[128,16384]{1,0:T(8,128)(2,1)} %all-gather.2.cloned.1.call-done, bf16[16384,2048]{1,0:T(8,128)(2,1)} %get-tuple-element.374), kind=kOutput, calls=%fused_computation.44.clone.1 | convolution fusion | flops 8590721024 | bytes 72876544 | tf_op jit(solution)/shard_map/while/body/eval_jaxpr/dot_general | solution.py:26
  410.4 30.0 %all-gather.2.cloned.1.call-done = bf16[128,16384]{1,0:T(8,128)(2,1)} async-done(((bf16[128,2048]{1,0:T(8,128)(2,1)}), bf16[128,16384]{1,0:T(8,128)(2,1)}) %all-gather.2.cloned.1.call-update) | async-done | bytes 4194320 | tf_op jit(solution)/shard_map/while/body/eval_jaxpr/all_gather | solution.py:25
  440.5 25.1 %fusion.35 = (f32[128]{0:T(128)S(1)}, f32[128,2048]{1,0:T(8,128)S(1)}) fusion(bf16[7,128,2048]{2,1,0:T(8,128)(2,1)} %get-tuple-element.375, s32[]{:T(128)S(6)} %copy.16, bf16[128,16384]{1,0:T(8,128)(2,1)} %all-gather.2.cloned.1.call-done, bf16[16384,2048]{1,0:T(8,128)(2,1)} %get-tuple-element.374), kind=kOutput, calls=%fused_computation.44.clone.1 | convolution fusion | flops 8590721024 | bytes 72876544 | tf_op jit(solution)/shard_map/while/body/eval_jaxpr/dot_general | solution.py:26
  479.2 30.4 %all-gather.2.cloned.1.call-done = bf16[128,16384]{1,0:T(8,128)(2,1)} async-done(((bf16[128,2048]{1,0:T(8,128)(2,1)}), bf16[128,16384]{1,0:T(8,128)(2,1)}) %all-gather.2.cloned.1.call-update) | async-done | bytes 4194320 | tf_op jit(solution)/shard_map/while/body/eval_jaxpr/all_gather | solution.py:25
  509.5 25.1 %fusion.35 = (f32[128]{0:T(128)S(1)}, f32[128,2048]{1,0:T(8,128)S(1)}) fusion(bf16[7,128,2048]{2,1,0:T(8,128)(2,1)} %get-tuple-element.375, s32[]{:T(128)S(6)} %copy.16, bf16[128,16384]{1,0:T(8,128)(2,1)} %all-gather.2.cloned.1.call-done, bf16[16384,2048]{1,0:T(8,128)(2,1)} %get-tuple-element.374), kind=kOutput, calls=%fused_computation.44.clone.1 | convolution fusion | flops 8590721024 | bytes 72876544 | tf_op jit(solution)/shard_map/while/body/eval_jaxpr/dot_general | solution.py:26
  549.7 488.7 %while.32 = (s32[]{:T(128)}, f32[128,2048]{1,0:T(8,128)S(1)}, bf16[6,128,2048]{2,1,0:T(8,128)(2,1)}, pred[6,128]{1,0:T(8,128)(4,1)S(1)}, bf16[6,128,2048]{2,1,0:...) while((s32[]{:T(128)}, f32[128,2048]{1,0:T(8,128)S(1)}, ...), condition=%wide.region_9.10_spmd.clone, body=%wide.region_7.9_spmd.clone.sunk | while | flops 8593342464 | bytes 109579960 | solution.py:43
  549.8 30.8 %fusion.39 = f32[128,16384]{1,0:T(8,128)} fusion(bf16[16384,2048]{1,0:T(8,128)(2,1)} %get-tuple-element.404, f32[128,2048]{1,0:T(8,128)S(1)} %get-tuple-element.389, f32[128]{0:T(128)S(1)} %fusion.38, bf16[6,128,2048]{2,1,0:T(8,128)(2,1)} %get-tuple-element.402, s32[]{:T(128)S(6)} %sub.9, pred[128]{0:T(512)(128)(4,1)S(1)} %get-tuple-element.349, ...), kind=kOutput, calls=%fused_computation.16.clone.1 | convolution fusion | flops 8591507456 | bytes 77070984 | tf_op jit(solution)/shard_map/while/body/eval_jaxpr/dot_general | solution.py:39
  582.7 46.5 %reduce-scatter.2.cloned.1.call-done = f32[128,2048]{1,0:T(8,128)} async-done(((f32[128,16384]{1,0:T(8,128)}), f32[128,2048]{1,0:T(8,128)}) %reduce-scatter.2.cloned.1.call-update) | async-done | bytes 1048592 | tf_op jit(solution)/shard_map/while/body/eval_jaxpr/reduce_scatter | solution.py:40
  630.7 30.8 %fusion.39 = f32[128,16384]{1,0:T(8,128)} fusion(bf16[16384,2048]{1,0:T(8,128)(2,1)} %get-tuple-element.404, f32[128,2048]{1,0:T(8,128)S(1)} %get-tuple-element.389, f32[128]{0:T(128)S(1)} %fusion.38, bf16[6,128,2048]{2,1,0:T(8,128)(2,1)} %get-tuple-element.402, s32[]{:T(128)S(6)} %sub.9, pred[128]{0:T(512)(128)(4,1)S(1)} %get-tuple-element.349, ...), kind=kOutput, calls=%fused_computation.16.clone.1 | convolution fusion | flops 8591507456 | bytes 77070984 | tf_op jit(solution)/shard_map/while/body/eval_jaxpr/dot_general | solution.py:39
  663.6 47.2 %reduce-scatter.2.cloned.1.call-done = f32[128,2048]{1,0:T(8,128)} async-done(((f32[128,16384]{1,0:T(8,128)}), f32[128,2048]{1,0:T(8,128)}) %reduce-scatter.2.cloned.1.call-update) | async-done | bytes 1048592 | tf_op jit(solution)/shard_map/while/body/eval_jaxpr/reduce_scatter | solution.py:40
  712.3 30.8 %fusion.39 = f32[128,16384]{1,0:T(8,128)} fusion(bf16[16384,2048]{1,0:T(8,128)(2,1)} %get-tuple-element.404, f32[128,2048]{1,0:T(8,128)S(1)} %get-tuple-element.389, f32[128]{0:T(128)S(1)} %fusion.38, bf16[6,128,2048]{2,1,0:T(8,128)(2,1)} %get-tuple-element.402, s32[]{:T(128)S(6)} %sub.9, pred[128]{0:T(512)(128)(4,1)S(1)} %get-tuple-element.349, ...), kind=kOutput, calls=%fused_computation.16.clone.1 | convolution fusion | flops 8591507456 | bytes 77070984 | tf_op jit(solution)/shard_map/while/body/eval_jaxpr/dot_general | solution.py:39
  745.2 47.2 %reduce-scatter.2.cloned.1.call-done = f32[128,2048]{1,0:T(8,128)} async-done(((f32[128,16384]{1,0:T(8,128)}), f32[128,2048]{1,0:T(8,128)}) %reduce-scatter.2.cloned.1.call-update) | async-done | bytes 1048592 | tf_op jit(solution)/shard_map/while/body/eval_jaxpr/reduce_scatter | solution.py:40
  793.8 30.8 %fusion.39 = f32[128,16384]{1,0:T(8,128)} fusion(bf16[16384,2048]{1,0:T(8,128)(2,1)} %get-tuple-element.404, f32[128,2048]{1,0:T(8,128)S(1)} %get-tuple-element.389, f32[128]{0:T(128)S(1)} %fusion.38, bf16[6,128,2048]{2,1,0:T(8,128)(2,1)} %get-tuple-element.402, s32[]{:T(128)S(6)} %sub.9, pred[128]{0:T(512)(128)(4,1)S(1)} %get-tuple-element.349, ...), kind=kOutput, calls=%fused_computation.16.clone.1 | convolution fusion | flops 8591507456 | bytes 77070984 | tf_op jit(solution)/shard_map/while/body/eval_jaxpr/dot_general | solution.py:39
  826.7 47.1 %reduce-scatter.2.cloned.1.call-done = f32[128,2048]{1,0:T(8,128)} async-done(((f32[128,16384]{1,0:T(8,128)}), f32[128,2048]{1,0:T(8,128)}) %reduce-scatter.2.cloned.1.call-update) | async-done | bytes 1048592 | tf_op jit(solution)/shard_map/while/body/eval_jaxpr/reduce_scatter | solution.py:40
  875.4 30.8 %fusion.39 = f32[128,16384]{1,0:T(8,128)} fusion(bf16[16384,2048]{1,0:T(8,128)(2,1)} %get-tuple-element.404, f32[128,2048]{1,0:T(8,128)S(1)} %get-tuple-element.389, f32[128]{0:T(128)S(1)} %fusion.38, bf16[6,128,2048]{2,1,0:T(8,128)(2,1)} %get-tuple-element.402, s32[]{:T(128)S(6)} %sub.9, pred[128]{0:T(512)(128)(4,1)S(1)} %get-tuple-element.349, ...), kind=kOutput, calls=%fused_computation.16.clone.1 | convolution fusion | flops 8591507456 | bytes 77070984 | tf_op jit(solution)/shard_map/while/body/eval_jaxpr/dot_general | solution.py:39
  908.3 47.1 %reduce-scatter.2.cloned.1.call-done = f32[128,2048]{1,0:T(8,128)} async-done(((f32[128,16384]{1,0:T(8,128)}), f32[128,2048]{1,0:T(8,128)}) %reduce-scatter.2.cloned.1.call-update) | async-done | bytes 1048592 | tf_op jit(solution)/shard_map/while/body/eval_jaxpr/reduce_scatter | solution.py:40
  956.9 30.8 %fusion.39 = f32[128,16384]{1,0:T(8,128)} fusion(bf16[16384,2048]{1,0:T(8,128)(2,1)} %get-tuple-element.404, f32[128,2048]{1,0:T(8,128)S(1)} %get-tuple-element.389, f32[128]{0:T(128)S(1)} %fusion.38, bf16[6,128,2048]{2,1,0:T(8,128)(2,1)} %get-tuple-element.402, s32[]{:T(128)S(6)} %sub.9, pred[128]{0:T(512)(128)(4,1)S(1)} %get-tuple-element.349, ...), kind=kOutput, calls=%fused_computation.16.clone.1 | convolution fusion | flops 8591507456 | bytes 77070984 | tf_op jit(solution)/shard_map/while/body/eval_jaxpr/dot_general | solution.py:39
  989.8 47.2 %reduce-scatter.2.cloned.1.call-done = f32[128,2048]{1,0:T(8,128)} async-done(((f32[128,16384]{1,0:T(8,128)}), f32[128,2048]{1,0:T(8,128)}) %reduce-scatter.2.cloned.1.call-update) | async-done | bytes 1048592 | tf_op jit(solution)/shard_map/while/body/eval_jaxpr/reduce_scatter | solution.py:40
  1038.4 12.8 %fusion.20 = f32[2048,2048,1]{1,0,2:T(8,128)} fusion(bf16[7,128,2048]{2,1,0:T(8,128)(2,1)} %get-tuple-element.186, bf16[6,128,2048]{2,1,0:T(8,128)(2,1)} %get-tuple-element.187), kind=kOutput, calls=%fused_computation.45 | convolution fusion | flops 6442450944 | bytes 23592960 | tf_op jit(solution)/shard_map/tbi,tbj->ij/dot_general | solution.py:45
  1051.2 17.1 %fusion.6 = f32[2048,2048]{1,0:T(8,128)} fusion(f32[2048,2048,1]{1,0,2:T(8,128)} %fusion.20, bf16[16384,2048]{1,0:T(8,128)(2,1)} %param.9, s32[]{:T(128)S(6)} %select_n.54, f32[128,2048]{1,0:T(8,128)S(1)} %get-tuple-element.188, bf16[8,128,2048]{2,1,0:T(8,128)(2,1)} %copy-done.2, f32[128]{0:T(128)S(1)} %slice_bitcast_fusion.4, ...), kind=kOutput, calls=%fused_computation.18 | convolution fusion | flops 1087635456 | bytes 44040836 | tf_op jit(solution)/shard_map/dot_general | solution.py:46
  (122 shorter events, 135.0 us)
Async XLA Ops:
  7.9 26.8 %copy-start.5 = (pred[7,128]{1,0:T(8,128)(4,1)}, pred[7,128]{1,0:T(8,128)(4,1)S(1)}, u32[]{:S(2)}) copy-start(pred[7,128]{1,0:T(8,128)(4,1)S(1)} %broadcast_compare_fusion) | copy-start | bytes 2692
  34.7 4.6 copy-start.4
  37.4 1.9 copy-start.2
  53.6 5.4 copy-start.3
  59.0 2.3 copy-start.6
  61.3 488.4 %copy-start = (f32[128,2048]{1,0:T(8,128)S(1)}, f32[128,2048]{1,0:T(8,128)}, u32[]{:S(2)}) copy-start(f32[128,2048]{1,0:T(8,128)} %custom-call) | copy-start | bytes 3145732
  61.3 488.4 %copy-start.7 = (pred[6,128]{1,0:T(8,128)(4,1)S(1)}, pred[6,128]{1,0:T(8,128)(4,1)}, u32[]{:S(2)}) copy-start(pred[6,128]{1,0:T(8,128)(4,1)} %slice.33) | copy-start | bytes 2308
  61.3 34.8 %all-gather.2.cloned.1.call-start = ((), (), s32[]{:S(2)}) async-start(), calls=%async_computation.1 | async-start | bytes 4718592 | tf_op jit(solution)/shard_map/while/body/eval_jaxpr/all_gather | solution.py:25
  133.6 31.6 %all-gather.2.cloned.1.call-start = ((), (), s32[]{:S(2)}) async-start(), calls=%async_computation.1 | async-start | bytes 4718592 | tf_op jit(solution)/shard_map/while/body/eval_jaxpr/all_gather | solution.py:25
  202.6 31.6 %all-gather.2.cloned.1.call-start = ((), (), s32[]{:S(2)}) async-start(), calls=%async_computation.1 | async-start | bytes 4718592 | tf_op jit(solution)/shard_map/while/body/eval_jaxpr/all_gather | solution.py:25
  271.7 31.3 %all-gather.2.cloned.1.call-start = ((), (), s32[]{:S(2)}) async-start(), calls=%async_computation.1 | async-start | bytes 4718592 | tf_op jit(solution)/shard_map/while/body/eval_jaxpr/all_gather | solution.py:25
  340.4 31.3 %all-gather.2.cloned.1.call-start = ((), (), s32[]{:S(2)}) async-start(), calls=%async_computation.1 | async-start | bytes 4718592 | tf_op jit(solution)/shard_map/while/body/eval_jaxpr/all_gather | solution.py:25
  409.2 31.3 %all-gather.2.cloned.1.call-start = ((), (), s32[]{:S(2)}) async-start(), calls=%async_computation.1 | async-start | bytes 4718592 | tf_op jit(solution)/shard_map/while/body/eval_jaxpr/all_gather | solution.py:25
  477.9 31.6 %all-gather.2.cloned.1.call-start = ((), (), s32[]{:S(2)}) async-start(), calls=%async_computation.1 | async-start | bytes 4718592 | tf_op jit(solution)/shard_map/while/body/eval_jaxpr/all_gather | solution.py:25
  547.0 2.7 copy-start.1
  549.7 79.5 %reduce-scatter.2.cloned.1.call-start = ((), (), s32[]{:S(2)}) async-start(), calls=%async_computation.2 | async-start | bytes 9437184 | tf_op jit(solution)/shard_map/while/body/eval_jaxpr/reduce_scatter | solution.py:40
  630.6 80.2 %reduce-scatter.2.cloned.1.call-start = ((), (), s32[]{:S(2)}) async-start(), calls=%async_computation.2 | async-start | bytes 9437184 | tf_op jit(solution)/shard_map/while/body/eval_jaxpr/reduce_scatter | solution.py:40
  712.1 80.2 %reduce-scatter.2.cloned.1.call-start = ((), (), s32[]{:S(2)}) async-start(), calls=%async_computation.2 | async-start | bytes 9437184 | tf_op jit(solution)/shard_map/while/body/eval_jaxpr/reduce_scatter | solution.py:40
  793.7 80.2 %reduce-scatter.2.cloned.1.call-start = ((), (), s32[]{:S(2)}) async-start(), calls=%async_computation.2 | async-start | bytes 9437184 | tf_op jit(solution)/shard_map/while/body/eval_jaxpr/reduce_scatter | solution.py:40
  875.3 80.2 %reduce-scatter.2.cloned.1.call-start = ((), (), s32[]{:S(2)}) async-start(), calls=%async_computation.2 | async-start | bytes 9437184 | tf_op jit(solution)/shard_map/while/body/eval_jaxpr/reduce_scatter | solution.py:40
  956.8 80.2 %reduce-scatter.2.cloned.1.call-start = ((), (), s32[]{:S(2)}) async-start(), calls=%async_computation.2 | async-start | bytes 9437184 | tf_op jit(solution)/shard_map/while/body/eval_jaxpr/reduce_scatter | solution.py:40
  1038.4 12.8 %copy-start.8 = (pred[128]{0:T(512)(128)(4,1)S(1)}, pred[128]{0:T(512)(128)(4,1)}, u32[]{:S(2)}) copy-start(pred[128]{0:T(512)(128)(4,1)} %slice_bitcast_fusion.3) | copy-start | bytes 388
Sparse Core Ops, SparseCore 0:
  64.3 31.7 all-gather.1
  136.6 28.5 all-gather.1
  205.6 28.5 all-gather.1
  274.4 28.5 all-gather.1
  343.1 28.5 all-gather.1
  411.9 28.5 all-gather.1
  481.0 28.5 all-gather.1
  580.8 48.3 reduce-scatter.1
  661.7 49.0 reduce-scatter.1
  743.2 49.0 reduce-scatter.1
  824.8 49.0 reduce-scatter.1
  906.3 49.0 reduce-scatter.1
  987.9 49.0 reduce-scatter.1
where the time goes:
time: 1080 us; the launch traced here: 1070 us
  waiting for transfers between devices  498 us (46%)
  matrix products  390 us (36%)
  blocking collectives  98.7 us (9%)
  other arithmetic  36.9 us (3%)
  local copies, waits for them, and re-layouts  36.1 us (3%)
  between operations  13.8 us (1%)
    reduce_scatter x6, waiting for transfers between devices, backward_step(): lax.psum_scatter(partial_sum, 'states', scatter_dimension=1, tiled=True)  282 us
    all_gather x7, waiting for transfers between devices, forward_step(): alpha_full = lax.all_gather(alpha_bf, 'states', axis=1, tiled=True)  215 us
    dot_general x6, matrix products, backward_step(): lax.dot_general(weight, trans_loc, (((1,), (1,)), ((), ())), preferred_el...  185 us
    dot_general x7, matrix products, forward_step(): jnp.dot(alpha_full, trans_loc, preferred_element_type=jnp.float32)  175 us
    psum x7, blocking collectives, forward_step(): norm_sum = lax.psum(jnp.sum(new_mass, axis=1), 'states')  84.7 us
    gather x1, local copies, waits for them, and re-layouts, local_run(): jnp.take(emit_loc, tokens_loc.T, axis=1)  24.2 us
  transfers between devices with their start and end apart: 13, of which 13 were waited for; matrix products, arithmetic and copies ran while one was open for 1% of the time, Pallas kernels for 0%

commit v1 on v0

v1 whole, which is shorter than its diff:
```python
import functools

import jax
import jax.numpy as jnp
from jax import lax
from jax.experimental import pallas as pl
from jax.experimental.pallas import tpu as pltpu
from jax.sharding import PartitionSpec as P

AXIS = "states"
LANES = 128
F32 = jnp.float32
BF16 = jnp.bfloat16


def _loop(n, body):
    def step(i, carry):
        body(i)
        return carry

    lax.fori_loop(0, n, step, 0)


def _recursion(caps, a_hbm, em_hbm, pi_ref, lcol_ref, lrow_ref, al_hbm, w_hbm, post_hbm, ll_ref,
               ring, al, acc, cur, emv, rcs, sbuf, csend, cbuf, wv, ost, sst, own, dbuf, trans, fin,
               ring_sem, em_sem, al_recv, own_send, part_send, on_send, c_send, c_recv, save_sem, post_sem,
               d_send, d_recv, s_send, t_recv, f_recv):
    nd = cbuf.shape[0]
    nx = nd // 2
    step_count, seqs, bs = em_hbm.shape
    hb = bs // 2
    slab = min(512, hb)
    tiles = bs // LANES
    g = lax.axis_index(AXIS)
    x, c = g // 2, g % 2

    def dev(dx, flip):
        return ((x + dx) % nx) * 2 + (c + flip) % 2

    partner, right, left = dev(0, 1), dev(1, 0), dev(nx - 1, 0)

    def remote(src, dst, send, recv, to):
        return pltpu.make_async_remote_copy(
            src_ref=src, dst_ref=dst, send_sem=send, recv_sem=recv,
            device_id={AXIS: to}, device_id_type=pl.DeviceIdType.MESH)

    def for_caps(t, fn):
        sizes = sorted(set(caps))
        if len(sizes) == 1:
            fn(sizes[0])
            return
        for tt in range(1, step_count):
            pl.when(t == tt)(functools.partial(fn, caps[tt - 1]))

    def fwd_row(group, i):
        if group == 0:
            src, half = dev(0, i // 2), i % 2
        elif group == 3:
            src, half = dev(2, i // 2), i % 2
        else:
            src, half = dev(nx - 1 - 2 * (i % 2), i // 2), (group - 1 + i % 2) % 2
        return src * bs + half * hb

    def bwd_row(group, i):
        q, flip = i // 2, 1 - i % 2
        if group == 0:
            src, half = dev(2, flip), q
        elif group == 3:
            src, half = dev(0, flip), q
        else:
            src, half = dev(1 + 2 * q, flip), (1 - q if group == 1 else q)
        return src * bs + half * hb

    def tile_copy(row, slot):
        return pltpu.make_async_copy(a_hbm.at[pl.ds(pl.multiple_of(row, hb), hb)], ring.at[slot], ring_sem.at[slot])

    def em_copy(t):
        return pltpu.make_async_copy(em_hbm.at[t], emv.at[t % 2], em_sem.at[t % 2])

    for grp in range(2):
        _loop(4, lambda i, grp=grp: tile_copy(fwd_row(grp, i), grp * 4 + i).start())
    em_copy(0).start()
    em_copy(1).start()

    barrier = pltpu.get_barrier_semaphore()
    for k in range(1, nd):
        pl.semaphore_signal(barrier, inc=1, device_id={AXIS: (g + k) % nd}, device_id_type=pl.DeviceIdType.MESH)
    pl.semaphore_wait(barrier, nd - 1)

    def rows_of(i):
        return pl.ds(pl.multiple_of(i * 16, 16), 16)

    def lane(k):
        return pl.ds(k * LANES, LANES)

    def inner(k):
        return (k * LANES) // hb, pl.ds((k * LANES) % hb, LANES)

    def weigh(t, first):
        def body(i):
            r = rows_of(i)
            total = jnp.zeros((16, LANES), F32)
            for k in range(tiles):
                e = emv[t % 2, r, lane(k)].astype(F32)
                mass = (pi_ref[:, lane(k)] * e) if first else acc[r, lane(k)] * e
                acc[r, lane(k)] = mass
                total = total + mass
            sbuf[r, :] = total

        _loop(seqs // 16, body)

    def normalise(t):
        row = jnp.sum(jnp.transpose(sbuf[...]), axis=0, keepdims=True)
        wide = jnp.broadcast_to(row, csend.shape)
        csend[...] = wide
        cbuf[g] = wide
        copies = [remote(csend, cbuf.at[g], c_send.at[k - 1], c_recv.at[g], (g + k) % nd) for k in range(1, nd)]
        for cp in copies:
            cp.start()
        for k in range(1, nd):
            frm = (g + k) % nd
            remote(csend, cbuf.at[frm], c_send.at[k - 1], c_recv.at[frm], frm).wait_recv()
        norm = cbuf[0, 0:1, :]
        for d in range(1, nd):
            norm = norm + cbuf[d, 0:1, :]
        rcs[t] = 1.0 / jnp.transpose(jnp.broadcast_to(norm, (LANES, LANES)))
        ll_ref[...] = ll_ref[...] + jnp.where(t < lrow_ref[...], jnp.log(jnp.broadcast_to(norm, ll_ref.shape)), 0.0)

        def body(i):
            r = rows_of(i)
            rc = rcs[t, r, :]
            live = t < lcol_ref[r, :]
            for k in range(tiles):
                h, col = inner(k)
                val = jnp.where(live, acc[r, lane(k)] * rc, cur[r, lane(k)])
                cur[r, lane(k)] = val
                al[0, h, r, col] = val.astype(BF16)

        _loop(seqs // 16, body)
        for cp in copies:
            cp.wait_send()

    ll_ref[...] = jnp.zeros_like(ll_ref)
    em_copy(0).wait()
    weigh(0, True)
    normalise(0)

    def own_copies(rows):
        m = pl.ds(0, rows)
        out = [remote(al.at[0, h, m], al.at[1, h, m], own_send.at[0, h], al_recv.at[1, h], partner) for h in (0, 1)]
        for h in (0, 1):
            out.append(remote(al.at[0, h, m], al.at[2, h, m], own_send.at[1, h], al_recv.at[2, h], right))
            out.append(remote(al.at[0, 1 - h, m], al.at[3, 1 - h, m], own_send.at[2, 1 - h], al_recv.at[3, 1 - h], left))
        return out

    def to_partner(slot, to_slot, half, rows):
        m = pl.ds(0, rows)
        return remote(al.at[slot, half, m], al.at[to_slot, half, m], part_send.at[slot, half], al_recv.at[to_slot, half], partner)

    def onward(s, rows):
        m = pl.ds(0, rows)
        return remote(al.at[2 + s, s, m], al.at[6, s, m], on_send.at[s], al_recv.at[6, s], dev(1 + (nx - 2) * s, 0))

    def arrived(slot, half, rows):
        m = pl.ds(0, rows)
        remote(al.at[slot, half, m], al.at[slot, half, m], part_send.at[slot, half], al_recv.at[slot, half], partner).wait_recv()

    def save_copies(t):
        return [pltpu.make_async_copy(al.at[0, h], al_hbm.at[t, :, pl.ds(h * hb, hb)], save_sem.at[h]) for h in (0, 1)]

    def multiply(slot, half, buf):
        lhs = al[slot, half]
        for n in range(bs // slab):
            cols = pl.ds(n * slab, slab)
            acc[:, cols] = acc[:, cols] + jnp.dot(lhs, ring[buf, :, cols], preferred_element_type=F32)

    def next_pass(t, group, i):
        slot = group * 4 + i

        @pl.when(t < step_count - 1)
        def _():
            tile_copy(fwd_row(group, i), slot).start()

        @pl.when(t == step_count - 1)
        def _():
            tile_copy(bwd_row(group, i), slot).start()

    def forward(idx):
        t = idx + 1
        for_caps(t, lambda rows: [cp.start() for cp in own_copies(rows)] and None)
        for cp in save_copies(t - 1):
            cp.start()

        @pl.when(t + 1 < step_count)
        def _():
            em_copy(t + 1).start()

        acc[...] = jnp.zeros_like(acc)

        def group0(i):
            slot, half = i // 2, i % 2
            pl.when(i >= 2)(lambda: for_caps(t, lambda rows: arrived(1, half, rows)))
            tile_copy(0, i).wait()
            multiply(slot, half, i)
            tile_copy(fwd_row(2, i), i).start()

        def group12(i, k):
            slot, half = 2 + i, (k + i % 2) % 2
            for_caps(t, lambda rows: arrived(slot, half, rows))

            @pl.when(i < 2)
            def _():
                def send(rows):
                    to_partner(slot, slot + 2, half, rows).start()
                    if k == 0:
                        onward(i, rows).start()

                for_caps(t, send)

            buf = 4 * (1 - k) + i
            tile_copy(0, buf).wait()
            multiply(slot, half, buf)
            if k == 0:
                tile_copy(fwd_row(3, i), buf).start()
            else:
                next_pass(t, 0, i)

        def group3(i):
            slot, half = 6 + i // 2, i % 2

            def ready(rows):
                arrived(slot, half, rows)
                pl.when(i < 2)(lambda: to_partner(6, 7, half, rows).start())

            for_caps(t, ready)
            tile_copy(0, 4 + i).wait()
            multiply(slot, half, 4 + i)
            next_pass(t, 1, i)

        _loop(4, group0)
        _loop(4, lambda i: group12(i, 0))
        _loop(4, lambda i: group12(i, 1))
        _loop(4, group3)

        def drained(rows):
            for cp in own_copies(rows):
                cp.wait_send()
            for half in (0, 1):
                to_partner(2, 4, half, rows).wait_send()
                to_partner(3, 5, half, rows).wait_send()
                to_partner(6, 7, half, rows).wait_send()
                onward(half, rows).wait_send()

        for_caps(t, drained)
        for cp in save_copies(t - 1):
            cp.wait()
        em_copy(t).wait()
        weigh(t, False)
        normalise(t)

    _loop(step_count - 1, forward)

    post_copy = pltpu.make_async_copy(cur, post_hbm, post_sem)
    post_copy.start()

    def weights(t):
        def body(i):
            r = rows_of(i)
            rc = rcs[t, r, :]
            live = t < lcol_ref[r, :]
            for k in range(tiles):
                h, col = inner(k)
                val = emv[t % 2, r, lane(k)].astype(F32) * own[h, r, col] * rc
                wv[r, lane(k)] = jnp.where(live, val, 0.0).astype(BF16)

        _loop(seqs // 16, body)

    def w_copy(t):
        return pltpu.make_async_copy(wv, w_hbm.at[t - 1], save_sem.at[0])

    def partial_sums(out, buf):
        for n in range(hb // slab):
            rows = pl.ds(n * slab, slab)
            out[:, rows] = lax.dot_general(wv[...], ring[buf, rows, :], (((1,), (1,)), ((), ())), preferred_element_type=F32)

    def add_into(out, *terms):
        def body(i):
            r = rows_of(i)
            val = out[r, :]
            for term in terms:
                val = val + term[r, :]
            out[r, :] = val

        _loop(seqs // 16, body)

    def to_core(p, q, rows):
        m = pl.ds(0, rows)
        return remote(ost.at[q, m], dbuf.at[p, m], d_send.at[q], d_recv.at[p], partner)

    def ring_copy(t, stage, q, rows):
        m, par, to = pl.ds(0, rows), t % 2, dev(1 + (nx - 2) * q, 0)
        if stage == 0:
            return remote(sst.at[q, m], trans.at[par, q, m], s_send.at[q], t_recv.at[par, q], to)
        half = 1 - q if stage == 1 else q
        p = stage * 2 + q
        return remote(sst.at[p, m], fin.at[par, q, half, m], s_send.at[p], f_recv.at[par, q, half], to)

    def backward(idx):
        t = step_count - 1 - idx
        par = t % 2
        weights(t)
        w_copy(t).start()

        @pl.when(t > 2)
        def _():
            em_copy(t - 2).start()

        def stage(n):
            def pair(q):
                p = n * 2 + q
                buf = 4 * (n % 2) + 2 * q
                if n > 0:
                    for_caps(t, lambda rows: to_core(p, q, rows).wait_send())
                tile_copy(0, buf).wait()
                partial_sums(ost.at[q], buf)
                for_caps(t, lambda rows: to_core(p, q, rows).start())

                def refill(i):
                    row = bwd_row((n + 2) % 4, 2 * q + i)
                    if n < 2:
                        tile_copy(row, buf + i).start()
                    else:
                        pl.when(t > 2)(lambda: tile_copy(row, buf + i).start())

                refill(0)
                tile_copy(0, buf + 1).wait()
                out = own.at[q] if n == 3 else sst.at[p]
                partial_sums(out, buf + 1)
                refill(1)
                for_caps(t, lambda rows: to_core(p, q, rows).wait_recv())
                if n == 2:
                    for_caps(t, lambda rows: ring_copy(t, 0, q, rows).wait_recv())
                    add_into(out, dbuf.at[p], trans.at[par, q])
                else:
                    add_into(out, dbuf.at[p])
                if n < 3:
                    for_caps(t, lambda rows: ring_copy(t, n, q, rows).start())

            _loop(2, pair)

        for n in range(4):
            stage(n)

        def landed(rows):
            for n in (1, 2):
                for q in (0, 1):
                    ring_copy(t, n, q, rows).wait_recv()

        for_caps(t, landed)

        def body(i):
            r = rows_of(i)
            live = t < lcol_ref[r, :]
            for k in range(tiles):
                h, col = inner(k)
                val = own[h, r, col] + fin[par, 0, h, r, col] + fin[par, 1, h, r, col]
                own[h, r, col] = jnp.where(live, val, 1.0)

        _loop(seqs // 16, body)

        def drained(rows):
            for q in (0, 1):
                to_core(6 + q, q, rows).wait_send()
                for n in range(3):
                    ring_copy(t, n, q, rows).wait_send()

        for_caps(t, drained)
        w_copy(t).wait()

        @pl.when(t > 2)
        def _():
            em_copy(t - 2).wait()

    own[...] = jnp.ones_like(own)
    _loop(step_count - 2, backward)
    weights(1)
    w_copy(1).start()
    w_copy(1).wait()
    post_copy.wait()


def _run_recursion(nd, caps, trans_loc, em, init_loc, lengths):
    step_count, seqs, bs = em.shape
    hb = bs // 2
    dma = pltpu.SemaphoreType.DMA
    lcol = jnp.broadcast_to(lengths[:, None], (seqs, LANES))
    lrow = jnp.broadcast_to(lengths[None, :], (8, seqs))
    vm, hbm = pl.BlockSpec(memory_space=pltpu.VMEM), pl.BlockSpec(memory_space=pl.ANY)
    scratch = [
        pltpu.VMEM((8, hb, bs), BF16),
        pltpu.VMEM((8, 2, seqs, hb), BF16),
        pltpu.VMEM((seqs, bs), F32),
        pltpu.VMEM((seqs, bs), F32),
        pltpu.VMEM((2, seqs, bs), BF16),
        pltpu.VMEM((step_count, seqs, LANES), F32),
        pltpu.VMEM((seqs, LANES), F32),
        pltpu.VMEM((8, seqs), F32),
        pltpu.VMEM((nd, 8, seqs), F32),
        pltpu.VMEM((seqs, bs), BF16),
        pltpu.VMEM((2, seqs, hb), F32),
        pltpu.VMEM((6, seqs, hb), F32),
        pltpu.VMEM((2, seqs, hb), F32),
        pltpu.VMEM((8, seqs, hb), F32),
        pltpu.VMEM((2, 2, seqs, hb), F32),
        pltpu.VMEM((2, 2, 2, seqs, hb), F32),
        dma((8,)), dma((2,)), dma((8, 2)), dma((3, 2)), dma((8, 2)), dma((2,)), dma((nd,)), dma((nd,)), dma((2,)), dma,
        dma((2,)), dma((8,)), dma((6,)), dma((2, 2)), dma((2, 2, 2)),
    ]
    return pl.pallas_call(
        functools.partial(_recursion, caps),
        name="recursion",
        out_shape=[
            jax.ShapeDtypeStruct((step_count - 1, seqs, bs), BF16),
            jax.ShapeDtypeStruct((step_count - 1, seqs, bs), BF16),
            jax.ShapeDtypeStruct((seqs, bs), F32),
            jax.ShapeDtypeStruct((8, seqs), F32),
        ],
        in_specs=[hbm, hbm, vm, vm, vm],
        out_specs=[hbm, hbm, hbm, vm],
        scratch_shapes=scratch,
        compiler_params=pltpu.CompilerParams(collective_id=0, has_side_effects=True, vmem_limit_bytes=66_000_000),
    )(trans_loc, em, init_loc[None, :], lcol, lrow)


def solution(mesh):
    nd = mesh.shape[AXIS]

    def local_run(trans_loc, emit_loc, init_loc, tokens_loc, lengths_loc):
        seqs, step_count = tokens_loc.shape
        bs = trans_loc.shape[1]
        em = jnp.take(emit_loc.T, tokens_loc.T.reshape(-1), axis=0, mode="clip").reshape(step_count, seqs, bs)
        caps = (seqs,) * (step_count - 1)
        alphas, ws, post, ll = _run_recursion(nd, caps, trans_loc, em, init_loc, lengths_loc)
        pair_sum = lax.dot_general(alphas.reshape(-1, bs), ws.reshape(-1, bs), (((0,), (0,)), ((), ())), preferred_element_type=F32)
        diag = lax.dynamic_slice_in_dim(trans_loc, lax.axis_index(AXIS) * bs, bs, axis=0)
        return ll[0], post, diag.astype(F32) * pair_sum

    return jax.shard_map(
        local_run,
        mesh=mesh,
        in_specs=(P(None, AXIS), P(AXIS, None), P(AXIS), P("seqs", None), P("seqs")),
        out_specs=(P("seqs"), P("seqs", AXIS), P(("seqs", AXIS), None)),
        check_vma=False,
    )
```

time: 1080 us -> 509 us (0.47)
  waiting for transfers between devices: 498 us -> 0 us
  Pallas kernels: 0 us -> 461 us
  matrix products: 390 us -> 16.5 us
  blocking collectives: 98.7 us -> 0 us
  other arithmetic: 36.9 us -> 0.69 us
  between operations: 13.8 us -> 0.65 us
    pallas_call x0 -> x1, Pallas kernels: none -> 461 us  [_run_recursion(): pl.pallas_call(functools.partial(_recursion, caps), name='recursion', out...]
    dot_general x15 -> x1, matrix products: 390 us -> 16.5 us  [local_run(): lax.dot_general(alphas.reshape(-1, bs), ws.reshape(-1, bs), (((0,), (0,))...]
    reduce_scatter x6 -> x0, waiting for transfers between devices: 282 us -> none  [backward_step(): lax.psum_scatter(partial_sum, 'states', scatter_dimension=1, tiled=True)]
    all_gather x7 -> x0, waiting for transfers between devices: 215 us -> none  [forward_step(): alpha_full = lax.all_gather(alpha_bf, 'states', axis=1, tiled=True)]
    psum x8 -> x0, blocking collectives: 98.7 us -> none  [the longest x7 84.7 us: forward_step(): norm_sum = lax.psum(jnp.sum(new_mass, axis=1), 'states')]
    dynamic_update_slice x13 -> x0, other arithmetic: 20.2 us -> none  [the longest x6 12.4 us: local_run(): lax.scan(backward_step, jnp.ones((seq_count, block_size), jnp.float32), (...]
  transfers between devices with their start and end apart: 13 -> 0, of which waited for: 13 -> 0; matrix products, arithmetic and copies ran while one was open for 1% -> 0% of each run, Pallas kernels for 0% -> 0%
where the time goes in v1:
time: 509 us; the launch traced here: 508 us
  Pallas kernels  461 us (91%)
  local copies, waits for them, and re-layouts  29 us (6%)
  matrix products  16.5 us (3%)
    pallas_call x1, Pallas kernels, _run_recursion(): pl.pallas_call(functools.partial(_recursion, caps), name='recursion', out...  461 us
    gather x1, local copies, waits for them, and re-layouts, local_run(): jnp.take(emit_loc.T, tokens_loc.T.reshape(-1), axis=0, mode='clip')  24.2 us
    dot_general x1, matrix products, local_run(): lax.dot_general(alphas.reshape(-1, bs), ws.reshape(-1, bs), (((0,), (0,))...  16.5 us

profile of v1, /device:TPU:81, one launch (start us, length us, event | category | flops | bytes accessed | tf_op | source)
XLA Modules:
  0.0 507.9 jit_solution(983339512090281857)
XLA Ops:
  0.6 0.7 bitcast_clamp_fusion
  1.3 1.2 broadcast_in_dim.22.lrow_ref
  2.6 1.4 broadcast_in_dim.21.lcol_ref
  3.9 24.2 %gather_fusion = bf16[1024,2048]{1,0:T(8,128)(2,1)} fusion(bf16[10000,2048]{1,0:T(8,128)(2,1)} %bitcast.13, s32[1024]{0:T(1024)S(1)} %bitcast_clamp_fusion), kind=kCustom, calls=%fused_computation | custom fusion | bytes 8392704 | tf_op jit(solution)/shard_map/jit(_take)/gather | solution.py:441
  28.2 461.1 %recursion.1 = (bf16[7,128,2048]{2,1,0:T(8,128)(2,1)}, bf16[7,128,2048]{2,1,0:T(8,128)(2,1)}, f32[128,2048]{1,0:T(8,128)}, f32[8,128]{1,0:T(8,128)}) custom-call(bf16[16384,2048]{1,0:T(8,128)(2,1)} %a_hbm.1, bf16[8,128,2048]{2,1,0:T(8,128)(2,1)} %bitcast.14, f32[1,2048]{1,0:T(1,128)} %bitcast.15, s32[128,128]{1,0:T(8,128)} %broadcast_in_dim.21.lcol_ref, ...), custom_call_target="tpu_custom_call" | custom-call | tf_op jit(solution)/shard_map/recursion/pallas_call | solution.py:419
  489.3 1.2 slice_bitcast_fusion
  490.5 0.0 copy-start
  490.5 16.5 %bitcast_multiply_fusion = f32[2048,2048]{1,0:T(8,128)} fusion(bf16[7,128,2048]{2,1,0:T(8,128)(2,1)} %get-tuple-element.9, bf16[7,128,2048]{2,1,0:T(8,128)(2,1)} %get-tuple-element.10, bf16[16384,2048]{1,0:T(8,128)(2,1)} %a_hbm.1, s32[]{:T(128)S(6)} %select_n.3), kind=kOutput, calls=%fused_computation.1 | convolution fusion | flops 7524581376 | bytes 32505860 | tf_op jit(solution)/shard_map/dot_general | solution.py:444
  507.0 0.0 copy-done
  507.0 1.0 copy.11
Async XLA Ops:
  490.5 16.5 %copy-start = (f32[128,2048]{1,0:T(8,128)S(1)}, f32[128,2048]{1,0:T(8,128)}, u32[]{:S(2)}) copy-start(f32[128,2048]{1,0:T(8,128)} %get-tuple-element.15) | copy-start | bytes 3145732

commit v2 on v1

--- a/solution.py
+++ b/solution.py
@@ -1,4 +1,5 @@
 import functools
+import math
 
 import jax
 import jax.numpy as jnp
@@ -22,8 +23,8 @@
 
 
 def _recursion(caps, a_hbm, em_hbm, pi_ref, lcol_ref, lrow_ref, al_hbm, w_hbm, post_hbm, ll_ref,
-               ring, al, acc, cur, emv, rcs, sbuf, csend, cbuf, wv, ost, sst, own, dbuf, trans, fin,
-               ring_sem, em_sem, al_recv, own_send, part_send, on_send, c_send, c_recv, save_sem, post_sem,
+               held, ring, al, acc, cur, emv, rcs, sbuf, csend, cbuf, wv, ost, sst, own, dbuf, trans, fin,
+               held_sem, ring_sem, em_sem, al_recv, own_send, part_send, on_send, c_send, c_recv, save_sem, post_sem,
                d_send, d_recv, s_send, t_recv, f_recv):
     nd = cbuf.shape[0]
     nx = nd // 2
@@ -31,6 +32,7 @@
     hb = bs // 2
     slab = min(512, hb)
     tiles = bs // LANES
+    kept = max(caps[1:])
     g = lax.axis_index(AXIS)
     x, c = g // 2, g % 2
 
@@ -44,12 +46,11 @@
             src_ref=src, dst_ref=dst, send_sem=send, recv_sem=recv,
             device_id={AXIS: to}, device_id_type=pl.DeviceIdType.MESH)
 
-    def for_caps(t, fn):
-        sizes = sorted(set(caps))
-        if len(sizes) == 1:
-            fn(sizes[0])
+    def for_caps(t, fn, first=1):
+        if len(set(caps)) == 1:
+            fn(caps[0])
             return
-        for tt in range(1, step_count):
+        for tt in range(first, step_count):
             pl.when(t == tt)(functools.partial(fn, caps[tt - 1]))
 
     def fwd_row(group, i):
@@ -74,13 +75,16 @@
     def tile_copy(row, slot):
         return pltpu.make_async_copy(a_hbm.at[pl.ds(pl.multiple_of(row, hb), hb)], ring.at[slot], ring_sem.at[slot])
 
+    def held_copy(i):
+        return pltpu.make_async_copy(a_hbm.at[pl.ds(pl.multiple_of(fwd_row(0, i), hb), hb)], held.at[i], held_sem.at[i])
+
     def em_copy(t):
         return pltpu.make_async_copy(em_hbm.at[t], emv.at[t % 2], em_sem.at[t % 2])
 
-    for grp in range(2):
-        _loop(4, lambda i, grp=grp: tile_copy(fwd_row(grp, i), grp * 4 + i).start())
     em_copy(0).start()
     em_copy(1).start()
+    _loop(4, lambda i: held_copy(i).start())
+    _loop(4, lambda i: tile_copy(fwd_row(1, i), i).start())
 
     barrier = pltpu.get_barrier_semaphore()
     for k in range(1, nd):
@@ -168,22 +172,20 @@
     def save_copies(t):
         return [pltpu.make_async_copy(al.at[0, h], al_hbm.at[t, :, pl.ds(h * hb, hb)], save_sem.at[h]) for h in (0, 1)]
 
-    def multiply(slot, half, buf):
+    def multiply(slot, half, tile):
         lhs = al[slot, half]
         for n in range(bs // slab):
             cols = pl.ds(n * slab, slab)
-            acc[:, cols] = acc[:, cols] + jnp.dot(lhs, ring[buf, :, cols], preferred_element_type=F32)
-
-    def next_pass(t, group, i):
-        slot = group * 4 + i
-
+            acc[:, cols] = acc[:, cols] + jnp.dot(lhs, tile[:, cols], preferred_element_type=F32)
+
+    def next_pass(t, i):
         @pl.when(t < step_count - 1)
         def _():
-            tile_copy(fwd_row(group, i), slot).start()
+            tile_copy(fwd_row(1, i), i).start()
 
         @pl.when(t == step_count - 1)
         def _():
-            tile_copy(bwd_row(group, i), slot).start()
+            tile_copy(bwd_row(0, i), i).start()
 
     def forward(idx):
         t = idx + 1
@@ -200,9 +202,8 @@
         def group0(i):
             slot, half = i // 2, i % 2
             pl.when(i >= 2)(lambda: for_caps(t, lambda rows: arrived(1, half, rows)))
-            tile_copy(0, i).wait()
-            multiply(slot, half, i)
-            tile_copy(fwd_row(2, i), i).start()
+            pl.when(t == 1)(lambda: held_copy(i).wait())
+            multiply(slot, half, held.at[i])
 
         def group12(i, k):
             slot, half = 2 + i, (k + i % 2) % 2
@@ -217,13 +218,9 @@
 
                 for_caps(t, send)
 
-            buf = 4 * (1 - k) + i
-            tile_copy(0, buf).wait()
-            multiply(slot, half, buf)
-            if k == 0:
-                tile_copy(fwd_row(3, i), buf).start()
-            else:
-                next_pass(t, 0, i)
+            tile_copy(0, i).wait()
+            multiply(slot, half, ring.at[i])
+            tile_copy(fwd_row(2 + k, i), i).start()
 
         def group3(i):
             slot, half = 6 + i // 2, i % 2
@@ -233,9 +230,9 @@
                 pl.when(i < 2)(lambda: to_partner(6, 7, half, rows).start())
 
             for_caps(t, ready)
-            tile_copy(0, 4 + i).wait()
-            multiply(slot, half, 4 + i)
-            next_pass(t, 1, i)
+            tile_copy(0, i).wait()
+            multiply(slot, half, ring.at[i])
+            next_pass(t, i)
 
         _loop(4, group0)
         _loop(4, lambda i: group12(i, 0))
@@ -278,20 +275,21 @@
     def w_copy(t):
         return pltpu.make_async_copy(wv, w_hbm.at[t - 1], save_sem.at[0])
 
-    def partial_sums(out, buf):
+    def partial_sums(out, tile):
         for n in range(hb // slab):
             rows = pl.ds(n * slab, slab)
-            out[:, rows] = lax.dot_general(wv[...], ring[buf, rows, :], (((1,), (1,)), ((), ())), preferred_element_type=F32)
+            out[0:kept, rows] = lax.dot_general(
+                wv[0:kept, :], tile[rows, :], (((1,), (1,)), ((), ())), preferred_element_type=F32)
 
     def add_into(out, *terms):
         def body(i):
-            r = rows_of(i)
+            r = pl.ds(pl.multiple_of(i * 8, 8), 8)
             val = out[r, :]
             for term in terms:
                 val = val + term[r, :]
             out[r, :] = val
 
-        _loop(seqs // 16, body)
+        _loop(kept // 8, body)
 
     def to_core(p, q, rows):
         m = pl.ds(0, rows)
@@ -318,33 +316,39 @@
         def stage(n):
             def pair(q):
                 p = n * 2 + q
-                buf = 4 * (n % 2) + 2 * q
+                buf = 2 * q
                 if n > 0:
-                    for_caps(t, lambda rows: to_core(p, q, rows).wait_send())
-                tile_copy(0, buf).wait()
-                partial_sums(ost.at[q], buf)
-                for_caps(t, lambda rows: to_core(p, q, rows).start())
+                    for_caps(t, lambda rows: to_core(p, q, rows).wait_send(), 2)
+                if n < 3:
+                    tile_copy(0, buf).wait()
+                    partial_sums(ost.at[q], ring.at[buf])
+                else:
+                    partial_sums(ost.at[q], held.at[2 + q])
+                for_caps(t, lambda rows: to_core(p, q, rows).start(), 2)
 
                 def refill(i):
-                    row = bwd_row((n + 2) % 4, 2 * q + i)
+                    row = bwd_row((n + 1) % 3, buf + i)
                     if n < 2:
                         tile_copy(row, buf + i).start()
-                    else:
+                    elif n == 2:
                         pl.when(t > 2)(lambda: tile_copy(row, buf + i).start())
 
                 refill(0)
-                tile_copy(0, buf + 1).wait()
                 out = own.at[q] if n == 3 else sst.at[p]
-                partial_sums(out, buf + 1)
+                if n < 3:
+                    tile_copy(0, buf + 1).wait()
+                    partial_sums(out, ring.at[buf + 1])
+                else:
+                    partial_sums(out, held.at[q])
                 refill(1)
-                for_caps(t, lambda rows: to_core(p, q, rows).wait_recv())
+                for_caps(t, lambda rows: to_core(p, q, rows).wait_recv(), 2)
                 if n == 2:
-                    for_caps(t, lambda rows: ring_copy(t, 0, q, rows).wait_recv())
+                    for_caps(t, lambda rows: ring_copy(t, 0, q, rows).wait_recv(), 2)
                     add_into(out, dbuf.at[p], trans.at[par, q])
                 else:
                     add_into(out, dbuf.at[p])
                 if n < 3:
-                    for_caps(t, lambda rows: ring_copy(t, n, q, rows).start())
+                    for_caps(t, lambda rows: ring_copy(t, n, q, rows).start(), 2)
 
             _loop(2, pair)
 
@@ -356,17 +360,17 @@
                 for q in (0, 1):
                     ring_copy(t, n, q, rows).wait_recv()
 
-        for_caps(t, landed)
+        for_caps(t, landed, 2)
 
         def body(i):
-            r = rows_of(i)
+            r = pl.ds(pl.multiple_of(i * 8, 8), 8)
             live = t < lcol_ref[r, :]
             for k in range(tiles):
                 h, col = inner(k)
                 val = own[h, r, col] + fin[par, 0, h, r, col] + fin[par, 1, h, r, col]
                 own[h, r, col] = jnp.where(live, val, 1.0)
 
-        _loop(seqs // 16, body)
+        _loop(kept // 8, body)
 
         def drained(rows):
             for q in (0, 1):
@@ -374,7 +378,7 @@
                 for n in range(3):
                     ring_copy(t, n, q, rows).wait_send()
 
-        for_caps(t, drained)
+        for_caps(t, drained, 2)
         w_copy(t).wait()
 
         @pl.when(t > 2)
@@ -389,15 +393,17 @@
     post_copy.wait()
 
 
-def _run_recursion(nd, caps, trans_loc, em, init_loc, lengths):
+def _run_recursion(nd, caps, ident, trans_loc, em, init_loc, lengths):
     step_count, seqs, bs = em.shape
     hb = bs // 2
+    kept = max(caps[1:])
     dma = pltpu.SemaphoreType.DMA
     lcol = jnp.broadcast_to(lengths[:, None], (seqs, LANES))
     lrow = jnp.broadcast_to(lengths[None, :], (8, seqs))
     vm, hbm = pl.BlockSpec(memory_space=pltpu.VMEM), pl.BlockSpec(memory_space=pl.ANY)
     scratch = [
-        pltpu.VMEM((8, hb, bs), BF16),
+        pltpu.VMEM((4, hb, bs), BF16),
+        pltpu.VMEM((4, hb, bs), BF16),
         pltpu.VMEM((8, 2, seqs, hb), BF16),
         pltpu.VMEM((seqs, bs), F32),
         pltpu.VMEM((seqs, bs), F32),
@@ -407,18 +413,18 @@
         pltpu.VMEM((8, seqs), F32),
         pltpu.VMEM((nd, 8, seqs), F32),
         pltpu.VMEM((seqs, bs), BF16),
+        pltpu.VMEM((2, kept, hb), F32),
+        pltpu.VMEM((6, kept, hb), F32),
         pltpu.VMEM((2, seqs, hb), F32),
-        pltpu.VMEM((6, seqs, hb), F32),
-        pltpu.VMEM((2, seqs, hb), F32),
-        pltpu.VMEM((8, seqs, hb), F32),
-        pltpu.VMEM((2, 2, seqs, hb), F32),
-        pltpu.VMEM((2, 2, 2, seqs, hb), F32),
-        dma((8,)), dma((2,)), dma((8, 2)), dma((3, 2)), dma((8, 2)), dma((2,)), dma((nd,)), dma((nd,)), dma((2,)), dma,
+        pltpu.VMEM((8, kept, hb), F32),
+        pltpu.VMEM((2, 2, kept, hb), F32),
+        pltpu.VMEM((2, 2, 2, kept, hb), F32),
+        dma((4,)), dma((4,)), dma((2,)), dma((8, 2)), dma((3, 2)), dma((8, 2)), dma((2,)), dma((nd,)), dma((nd,)), dma((2,)), dma,
         dma((2,)), dma((8,)), dma((6,)), dma((2, 2)), dma((2, 2, 2)),
     ]
     return pl.pallas_call(
         functools.partial(_recursion, caps),
-        name="recursion",
+        name=f"recursion{ident}",
         out_shape=[
             jax.ShapeDtypeStruct((step_count - 1, seqs, bs), BF16),
             jax.ShapeDtypeStruct((step_count - 1, seqs, bs), BF16),
@@ -428,8 +434,17 @@
         in_specs=[hbm, hbm, vm, vm, vm],
         out_specs=[hbm, hbm, hbm, vm],
         scratch_shapes=scratch,
-        compiler_params=pltpu.CompilerParams(collective_id=0, has_side_effects=True, vmem_limit_bytes=66_000_000),
+        compiler_params=pltpu.CompilerParams(collective_id=ident, has_side_effects=True, vmem_limit_bytes=66_000_000),
     )(trans_loc, em, init_loc[None, :], lcol, lrow)
+
+
+def _capacities(seqs, step_count):
+    caps = []
+    for t in range(1, step_count):
+        live = (step_count - t) / step_count
+        room = 3.1 * math.sqrt((seqs - 1) * live * (1 - live))
+        caps.append(min(seqs, 8 * math.ceil(((seqs - 1) * live + 1 + room) / 8)))
+    return tuple(caps)
 
 
 def solution(mesh):
@@ -438,12 +453,28 @@
     def local_run(trans_loc, emit_loc, init_loc, tokens_loc, lengths_loc):
         seqs, step_count = tokens_loc.shape
         bs = trans_loc.shape[1]
-        em = jnp.take(emit_loc.T, tokens_loc.T.reshape(-1), axis=0, mode="clip").reshape(step_count, seqs, bs)
-        caps = (seqs,) * (step_count - 1)
-        alphas, ws, post, ll = _run_recursion(nd, caps, trans_loc, em, init_loc, lengths_loc)
+        ids = jnp.arange(seqs)
+        ahead = (lengths_loc[:, None] > lengths_loc[None, :]) | (
+            (lengths_loc[:, None] == lengths_loc[None, :]) & (ids[:, None] < ids[None, :]))
+        rank = jnp.sum(ahead.astype(jnp.int32), axis=0)
+        pick = (rank[None, :] == ids[:, None]).astype(jnp.int32)
+        tokens = jnp.sum(pick[:, :, None] * tokens_loc[None, :, :], axis=1)
+        lengths = jnp.sum(pick * lengths_loc[None, :], axis=1)
+
+        em = jnp.take(emit_loc.T, tokens.T.reshape(-1), axis=0, mode="clip").reshape(step_count, seqs, bs)
+        caps = _capacities(seqs, step_count)
+        fits = True
+        for t in range(1, step_count):
+            fits = fits & (jnp.sum((lengths_loc > t).astype(jnp.int32)) <= caps[t - 1])
+        alphas, ws, post, ll = lax.cond(
+            fits,
+            functools.partial(_run_recursion, nd, caps, 0),
+            functools.partial(_run_recursion, nd, (seqs,) * (step_count - 1), 1),
+            trans_loc, em, init_loc, lengths)
         pair_sum = lax.dot_general(alphas.reshape(-1, bs), ws.reshape(-1, bs), (((0,), (0,)), ((), ())), preferred_element_type=F32)
         diag = lax.dynamic_slice_in_dim(trans_loc, lax.axis_index(AXIS) * bs, bs, axis=0)
-        return ll[0], post, diag.astype(F32) * pair_sum
+        loglik = jnp.sum(pick.astype(F32) * ll[0][:, None], axis=0)
+        return loglik, jnp.take(post, rank, axis=0, mode="clip"), diag.astype(F32) * pair_sum
 
     return jax.shard_map(
         local_run,

time: 509 us -> 418 us (0.82)
  Pallas kernels: 461 us -> 360 us
  other arithmetic: 0.69 us -> 6.62 us
    pallas_call x1, Pallas kernels: 461 us -> 360 us  [_run_recursion(): pl.pallas_call(functools.partial(_recursion, caps), name=f'recursion{iden...]
    reduce_sum x0 -> x5, other arithmetic: none -> 6.59 us  [the longest x1 2.92 us: local_run(): tokens = jnp.sum(pick[:, :, None] * tokens_loc[None, :, :], axis=1)]
    gather x1 -> x2, local copies, waits for them, and re-layouts: 24.2 us -> 27.9 us  [the longest x1 24.3 us: local_run(): jnp.take(emit_loc.T, tokens.T.reshape(-1), axis=0, mode='clip')]
where the time goes in v2:
time: 418 us
  Pallas kernels  360 us (86%)
  local copies, waits for them, and re-layouts  29.2 us (7%)
  matrix products  16.4 us (4%)
  other arithmetic  6.62 us (2%)
  between operations  5.16 us (1%)
    pallas_call x1, Pallas kernels, _run_recursion(): pl.pallas_call(functools.partial(_recursion, caps), name=f'recursion{iden...  360 us
    gather x1, local copies, waits for them, and re-layouts, local_run(): jnp.take(emit_loc.T, tokens.T.reshape(-1), axis=0, mode='clip')  24.3 us
    dot_general x1, matrix products, local_run(): lax.dot_general(alphas.reshape(-1, bs), ws.reshape(-1, bs), (((0,), (0,))...  16.4 us

profile of v2, /device:TPU:81, one launch (start us, length us, event | category | flops | bytes accessed | tf_op | source)
XLA Modules:
  0.0 417.5 jit_solution(11955538435114068802)
XLA Ops:
  0.6 0.8 convert_reduce_fusion
  1.5 0.8 select_reduce_fusion
  2.2 1.5 fusion.9
  8.2 2.9 multiply_reduce_fusion
  11.2 0.0 copy-start
  11.2 24.3 %gather_fusion = bf16[1024,2048]{1,0:T(8,128)(2,1)} fusion(bf16[10000,2048]{1,0:T(8,128)(2,1)} %bitcast.15, s32[1024]{0:T(1024)S(1)} %bitcast_clamp_fusion), kind=kCustom, calls=%fused_computation | custom fusion | bytes 8392704 | tf_op jit(solution)/shard_map/jit(_take)/gather | solution.py:464
  35.5 0.0 copy-done
  35.5 361.4 %conditional.1 = ((bf16[7,128,2048]{2,1,0:T(8,128)(2,1)}, bf16[7,128,2048]{2,1,0:T(8,128)(2,1)}, f32[128,2048]{1,0:T(8,128)}, f32[8,128]{1,0:T(8,128)S(1)})) conditional(s32[]{:T(128)} %convert_element_type.50, (f32[2048]{0:T(1024)S(1)}, s32[128]{0:T(128)S(1)}, bf16[16384,2048]{1,0:T(8,128)(2,1)}, bf16[8,128,2048]{2,1,0:T(8,128)(2,1)}) %tuple.28, ...), branch_computations={%region_10.11_spmd, %region_11.12_spmd} | conditional | bytes 70664 | solution.py:469
  35.5 0.6 broadcast_in_dim.16.lrow_ref
  36.1 0.7 broadcast_in_dim.13.lcol_ref
  36.8 359.9 %recursion0.1 = (bf16[7,128,2048]{2,1,0:T(8,128)(2,1)}, bf16[7,128,2048]{2,1,0:T(8,128)(2,1)}, f32[128,2048]{1,0:T(8,128)}, f32[8,128]{1,0:T(8,128)S(1)}) custom-call(bf16[16384,2048]{1,0:T(8,128)(2,1)} %get-tuple-element.20.a_hbm, bf16[8,128,2048]{2,1,0:T(8,128)(2,1)} %get-tuple-element.21.em_hbm, f32[1,2048]{1,0:T(1,128)S(1)} %bitcast.18, ...), custom_call_target="tpu_custom_call" | custom-call | tf_op jit(solution)/shard_map/cond/branch_1_fun/recursion0/pallas_call | solution.py:425
  396.9 0.6 multiply_reduce_fusion.1
  397.5 3.6 gather_fusion.1
  401.1 16.4 %bitcast_multiply_fusion = f32[2048,2048]{1,0:T(8,128)} fusion(bf16[7,128,2048]{2,1,0:T(8,128)(2,1)} %get-tuple-element.33, bf16[7,128,2048]{2,1,0:T(8,128)(2,1)} %get-tuple-element.34, bf16[16384,2048]{1,0:T(8,128)(2,1)} %param.7, s32[]{:T(128)S(6)} %select_n.3), kind=kOutput, calls=%fused_computation.2 | convolution fusion | flops 7524581376 | bytes 32505860 | tf_op jit(solution)/shard_map/dot_general | solution.py:474
  (5 shorter events, 0.1 us)
Async XLA Ops:
  11.2 24.3 %copy-start = (f32[2048]{0:T(1024)S(1)}, f32[2048]{0:T(1024)}, u32[]{:S(2)}) copy-start(f32[2048]{0:T(1024)} %param.9) | copy-start | bytes 24580

commit v3 on v2

--- a/solution.py
+++ b/solution.py
@@ -30,6 +30,7 @@
     nx = nd // 2
     step_count, seqs, bs = em_hbm.shape
     hb = bs // 2
+    firsts = [sum(caps[:t]) for t in range(step_count)]
     slab = min(512, hb)
     tiles = bs // LANES
     kept = max(caps[1:])
@@ -45,6 +46,10 @@
         return pltpu.make_async_remote_copy(
             src_ref=src, dst_ref=dst, send_sem=send, recv_sem=recv,
             device_id={AXIS: to}, device_id_type=pl.DeviceIdType.MESH)
+
+    def for_each(t, fn):
+        for tt in range(1, step_count):
+            pl.when(t == tt)(functools.partial(fn, tt, caps[tt - 1]))
 
     def for_caps(t, fn, first=1):
         if len(set(caps)) == 1:
@@ -169,8 +174,10 @@
         m = pl.ds(0, rows)
         remote(al.at[slot, half, m], al.at[slot, half, m], part_send.at[slot, half], al_recv.at[slot, half], partner).wait_recv()
 
-    def save_copies(t):
-        return [pltpu.make_async_copy(al.at[0, h], al_hbm.at[t, :, pl.ds(h * hb, hb)], save_sem.at[h]) for h in (0, 1)]
+    def save_copies(t, rows):
+        to = pl.ds(firsts[t - 1], rows)
+        return [pltpu.make_async_copy(al.at[0, h, pl.ds(0, rows)], al_hbm.at[to, pl.ds(h * hb, hb)], save_sem.at[h])
+                for h in (0, 1)]
 
     def multiply(slot, half, tile):
         lhs = al[slot, half]
@@ -190,8 +197,7 @@
     def forward(idx):
         t = idx + 1
         for_caps(t, lambda rows: [cp.start() for cp in own_copies(rows)] and None)
-        for cp in save_copies(t - 1):
-            cp.start()
+        for_each(t, lambda tt, rows: [cp.start() for cp in save_copies(tt, rows)] and None)
 
         @pl.when(t + 1 < step_count)
         def _():
@@ -249,8 +255,7 @@
                 onward(half, rows).wait_send()
 
         for_caps(t, drained)
-        for cp in save_copies(t - 1):
-            cp.wait()
+        for_each(t, lambda tt, rows: [cp.wait() for cp in save_copies(tt, rows)] and None)
         em_copy(t).wait()
         weigh(t, False)
         normalise(t)
@@ -272,8 +277,8 @@
 
         _loop(seqs // 16, body)
 
-    def w_copy(t):
-        return pltpu.make_async_copy(wv, w_hbm.at[t - 1], save_sem.at[0])
+    def w_copy(t, rows):
+        return pltpu.make_async_copy(wv.at[pl.ds(0, rows)], w_hbm.at[pl.ds(firsts[t - 1], rows)], save_sem.at[0])
 
     def partial_sums(out, tile):
         for n in range(hb // slab):
@@ -307,7 +312,7 @@
         t = step_count - 1 - idx
         par = t % 2
         weights(t)
-        w_copy(t).start()
+        for_each(t, lambda tt, rows: w_copy(tt, rows).start())
 
         @pl.when(t > 2)
         def _():
@@ -379,7 +384,7 @@
                     ring_copy(t, n, q, rows).wait_send()
 
         for_caps(t, drained, 2)
-        w_copy(t).wait()
+        for_each(t, lambda tt, rows: w_copy(tt, rows).wait())
 
         @pl.when(t > 2)
         def _():
@@ -388,18 +393,16 @@
     own[...] = jnp.ones_like(own)
     _loop(step_count - 2, backward)
     weights(1)
-    w_copy(1).start()
-    w_copy(1).wait()
+    w_copy(1, caps[0]).start()
+    w_copy(1, caps[0]).wait()
     post_copy.wait()
 
 
-def _run_recursion(nd, caps, ident, trans_loc, em, init_loc, lengths):
+def _run_recursion(nd, caps, ident, trans_loc, em, init_loc, lcol, lrow):
     step_count, seqs, bs = em.shape
     hb = bs // 2
     kept = max(caps[1:])
     dma = pltpu.SemaphoreType.DMA
-    lcol = jnp.broadcast_to(lengths[:, None], (seqs, LANES))
-    lrow = jnp.broadcast_to(lengths[None, :], (8, seqs))
     vm, hbm = pl.BlockSpec(memory_space=pltpu.VMEM), pl.BlockSpec(memory_space=pl.ANY)
     scratch = [
         pltpu.VMEM((4, hb, bs), BF16),
@@ -426,8 +429,8 @@
         functools.partial(_recursion, caps),
         name=f"recursion{ident}",
         out_shape=[
-            jax.ShapeDtypeStruct((step_count - 1, seqs, bs), BF16),
-            jax.ShapeDtypeStruct((step_count - 1, seqs, bs), BF16),
+            jax.ShapeDtypeStruct((sum(caps), bs), BF16),
+            jax.ShapeDtypeStruct((sum(caps), bs), BF16),
             jax.ShapeDtypeStruct((seqs, bs), F32),
             jax.ShapeDtypeStruct((8, seqs), F32),
         ],
@@ -438,6 +441,177 @@
     )(trans_loc, em, init_loc[None, :], lcol, lrow)
 
 
+def _prepare(caps, tok_ref, len_ref, emt_hbm, em_hbm, lcol_ref, lrow_ref, rank_ref, fits_ref,
+             table, stable, picked, blocks, stage, table_sem, block_sem, stage_sem):
+    step_count, seqs, bs = em_hbm.shape
+    deep = blocks.shape[0]
+    part = 32
+    slab = min(512, bs)
+    sub = lax.broadcasted_iota(jnp.int32, (seqs, LANES), 0)
+    lan = lax.broadcasted_iota(jnp.int32, (seqs, LANES), 1)
+    across = jnp.broadcast_to(len_ref[...].astype(F32), (seqs, seqs))
+    down = jnp.transpose(across)
+    ahead = (down > across) | ((down == across) & (sub < lan))
+    rank = jnp.sum(jnp.where(ahead, 1.0, 0.0), axis=0, keepdims=True)
+    rank_ref[...] = jnp.broadcast_to(rank, rank_ref.shape)
+    pick = rank == sub.astype(F32)
+    lcol = jnp.broadcast_to(jnp.sum(jnp.where(pick, across, 0.0), axis=1, keepdims=True), (seqs, LANES))
+    lcol_ref[...] = lcol.astype(jnp.int32)
+    lrow_ref[...] = jnp.transpose(lcol)[0:8].astype(jnp.int32)
+    mat = jnp.zeros((seqs, LANES), F32)
+    for t in range(step_count):
+        tok = jnp.sum(jnp.where(pick, tok_ref[t : t + 1, :].astype(F32), 0.0), axis=1, keepdims=True)
+        tok = jnp.broadcast_to(tok, (seqs, LANES))
+        mat = jnp.where(lan == t, tok, mat)
+        picked[t] = tok.astype(jnp.int32) & 7
+    table[0:8] = jnp.transpose(mat)[0:8].astype(jnp.int32)
+    alive = jnp.sum(jnp.where(across[0:8] > sub[0:8].astype(F32), 1.0, 0.0), axis=1, keepdims=True)
+    table[8:16] = jnp.broadcast_to(alive, (8, LANES)).astype(jnp.int32)
+    copy = pltpu.make_async_copy(table, stable, table_sem)
+    copy.start()
+    copy.wait()
+    fits = jnp.int32(1)
+    for t in range(1, step_count):
+        fits = jnp.where(stable[8 + t, 0] > caps[t - 1], 0, fits)
+    fits_ref[0] = fits
+
+    def parts(t):
+        return (stable[8 + t, 0] + (part - 1)) // part
+
+    def fetch(t):
+        def body(p, carry):
+            for k in range(part):
+                s = p * part + k
+                pltpu.make_async_copy(emt_hbm.at[stable[t, s] >> 3], blocks.at[t % deep, s], block_sem.at[t % deep]).start()
+            return carry
+
+        lax.fori_loop(0, parts(t), body, 0)
+
+    def landed(t):
+        def body(p, carry):
+            pltpu.make_async_copy(emt_hbm.at[pl.ds(0, part)], blocks.at[t % deep, pl.ds(0, part)], block_sem.at[t % deep]).wait()
+            return carry
+
+        lax.fori_loop(0, parts(t), body, 0)
+
+    def select(t):
+        def body(p, carry):
+            r = pl.ds(pl.multiple_of(p * part, part), part)
+            at = picked[t, r, :] + 8 * sub[0:part]
+            one = jnp.concatenate([jnp.where(lan[0:part] + off == at, 1.0, 0.0) for off in (0, LANES)], axis=1).astype(BF16)
+            for n in range(bs // slab):
+                cols = pl.ds(n * slab, slab)
+                rows = blocks[t % deep, r, :, cols].reshape(part * 8, slab)
+                stage[t % 2, r, cols] = jnp.dot(one, rows, preferred_element_type=F32).astype(BF16)
+            return carry
+
+        lax.fori_loop(0, parts(t), body, 0)
+
+    def out_copy(t):
+        return pltpu.make_async_copy(stage.at[t % 2], em_hbm.at[t], stage_sem.at[t % 2])
+
+    for t in range(min(deep, step_count)):
+        fetch(t)
+    for t in range(step_count):
+        if t >= 2:
+            out_copy(t - 2).wait()
+        landed(t)
+        select(t)
+        out_copy(t).start()
+        if t + deep < step_count:
+            fetch(t + deep)
+    for t in range(step_count - 2, step_count):
+        out_copy(t).wait()
+
+
+def _run_prepare(caps, tokens, lengths, emit_loc):
+    bs, symbols = emit_loc.shape
+    seqs, step_count = tokens.shape
+    dma = pltpu.SemaphoreType.DMA
+    vm, hbm = pl.BlockSpec(memory_space=pltpu.VMEM), pl.BlockSpec(memory_space=pl.ANY)
+    return pl.pallas_call(
+        functools.partial(_prepare, caps),
+        name="prepare",
+        out_shape=[
+            jax.ShapeDtypeStruct((step_count, seqs, bs), BF16),
+            jax.ShapeDtypeStruct((seqs, LANES), jnp.int32),
+            jax.ShapeDtypeStruct((8, seqs), jnp.int32),
+            jax.ShapeDtypeStruct((8, seqs), F32),
+            jax.ShapeDtypeStruct((1,), jnp.int32),
+        ],
+        in_specs=[vm, vm, hbm],
+        out_specs=[hbm, vm, vm, vm, pl.BlockSpec(memory_space=pltpu.SMEM)],
+        scratch_shapes=[
+            pltpu.VMEM((16, LANES), jnp.int32),
+            pltpu.SMEM((16, LANES), jnp.int32),
+            pltpu.VMEM((step_count, seqs, LANES), jnp.int32),
+            pltpu.VMEM((4, seqs, 8, bs), BF16),
+            pltpu.VMEM((2, seqs, bs), BF16),
+            dma, dma((4,)), dma((2,)),
+        ],
+        compiler_params=pltpu.CompilerParams(vmem_limit_bytes=60_000_000),
+    )(tokens.T, lengths[None, :], emit_loc.T.reshape(symbols // 8, 8, bs))
+
+
+def _counts(block_ref, alpha_ref, w_ref, diag_ref, post_ref, ll_ref, rank_ref, counts_ref, posterior_ref, loglik_ref):
+    bs = w_ref.shape[1]
+    slab = min(512, bs)
+    lhs = alpha_ref[...]
+    for n in range(bs // slab):
+        cols = pl.ds(n * slab, slab)
+        sums = lax.dot_general(lhs, w_ref[:, cols], (((0,), (0,)), ((), ())), preferred_element_type=F32)
+        counts_ref[:, cols] = diag_ref[:, cols].astype(F32) * sums
+    seqs = post_ref.shape[0]
+    rank = jnp.broadcast_to(rank_ref[0:1, :], (seqs, seqs))
+    sub = lax.broadcasted_iota(jnp.int32, (seqs, seqs), 0).astype(F32)
+    lan = lax.broadcasted_iota(jnp.int32, (seqs, seqs), 1).astype(F32)
+    back = jnp.where(jnp.transpose(rank) == lan, 1.0, 0.0).astype(BF16)
+    rest = post_ref[...]
+    total = jnp.zeros(posterior_ref.shape, F32)
+    for _ in range(3):
+        head = rest.astype(BF16)
+        rest = rest - head.astype(F32)
+        total = total + jnp.dot(back, head, preferred_element_type=F32)
+    posterior_ref[...] = total
+    lls = jnp.transpose(jnp.broadcast_to(ll_ref[0:1, :], (seqs, seqs)))
+    loglik_ref[...] = jnp.sum(jnp.where(rank == sub, lls, 0.0), axis=0, keepdims=True)
+
+
+def _run_counts(alphas, ws, trans_loc, post, ll, rank):
+    rows, bs = alphas.shape
+    seqs = post.shape[0]
+    tile = min(256, bs)
+    steps = bs // tile
+    block = lax.axis_index(AXIS).astype(jnp.int32)[None]
+    return pl.pallas_call(
+        _counts,
+        name="counts",
+        out_shape=[
+            jax.ShapeDtypeStruct((bs, bs), F32),
+            jax.ShapeDtypeStruct((seqs, bs), F32),
+            jax.ShapeDtypeStruct((1, seqs), F32),
+        ],
+        grid_spec=pltpu.PrefetchScalarGridSpec(
+            num_scalar_prefetch=1,
+            grid=(steps,),
+            in_specs=[
+                pl.BlockSpec((rows, tile), lambda i, b: (0, i)),
+                pl.BlockSpec((rows, bs), lambda i, b: (0, 0)),
+                pl.BlockSpec((tile, bs), lambda i, b: (b[0] * steps + i, 0)),
+                pl.BlockSpec((seqs, tile), lambda i, b: (0, i)),
+                pl.BlockSpec((8, seqs), lambda i, b: (0, 0)),
+                pl.BlockSpec((8, seqs), lambda i, b: (0, 0)),
+            ],
+            out_specs=[
+                pl.BlockSpec((tile, bs), lambda i, b: (i, 0)),
+                pl.BlockSpec((seqs, tile), lambda i, b: (0, i)),
+                pl.BlockSpec((1, seqs), lambda i, b: (0, 0)),
+            ],
+        ),
+        compiler_params=pltpu.CompilerParams(vmem_limit_bytes=60_000_000),
+    )(block, alphas, ws, trans_loc, post, ll, rank)
+
+
 def _capacities(seqs, step_count):
     caps = []
     for t in range(1, step_count):
@@ -452,29 +626,19 @@
 
     def local_run(trans_loc, emit_loc, init_loc, tokens_loc, lengths_loc):
         seqs, step_count = tokens_loc.shape
-        bs = trans_loc.shape[1]
-        ids = jnp.arange(seqs)
-        ahead = (lengths_loc[:, None] > lengths_loc[None, :]) | (
-            (lengths_loc[:, None] == lengths_loc[None, :]) & (ids[:, None] < ids[None, :]))
-        rank = jnp.sum(ahead.astype(jnp.int32), axis=0)
-        pick = (rank[None, :] == ids[:, None]).astype(jnp.int32)
-        tokens = jnp.sum(pick[:, :, None] * tokens_loc[None, :, :], axis=1)
-        lengths = jnp.sum(pick * lengths_loc[None, :], axis=1)
-
-        em = jnp.take(emit_loc.T, tokens.T.reshape(-1), axis=0, mode="clip").reshape(step_count, seqs, bs)
         caps = _capacities(seqs, step_count)
-        fits = True
-        for t in range(1, step_count):
-            fits = fits & (jnp.sum((lengths_loc > t).astype(jnp.int32)) <= caps[t - 1])
-        alphas, ws, post, ll = lax.cond(
-            fits,
-            functools.partial(_run_recursion, nd, caps, 0),
-            functools.partial(_run_recursion, nd, (seqs,) * (step_count - 1), 1),
-            trans_loc, em, init_loc, lengths)
-        pair_sum = lax.dot_general(alphas.reshape(-1, bs), ws.reshape(-1, bs), (((0,), (0,)), ((), ())), preferred_element_type=F32)
-        diag = lax.dynamic_slice_in_dim(trans_loc, lax.axis_index(AXIS) * bs, bs, axis=0)
-        loglik = jnp.sum(pick.astype(F32) * ll[0][:, None], axis=0)
-        return loglik, jnp.take(post, rank, axis=0, mode="clip"), diag.astype(F32) * pair_sum
+        em, lcol, lrow, rank, fits = _run_prepare(caps, tokens_loc, lengths_loc, emit_loc)
+
+        def run(caps, ident, trans, em, init, lcol, lrow, rank):
+            alphas, ws, post, ll = _run_recursion(nd, caps, ident, trans, em, init, lcol, lrow)
+            return _run_counts(alphas, ws, trans, post, ll, rank)
+
+        counts, posterior, loglik = lax.cond(
+            fits[0] == 1,
+            functools.partial(run, caps, 0),
+            functools.partial(run, (seqs,) * (step_count - 1), 1),
+            trans_loc, em, init_loc, lcol, lrow, rank)
+        return loglik[0], posterior, counts
 
     return jax.shard_map(
         local_run,

time: 418 us -> 394 us (0.943)
  Pallas kernels: 360 us -> 392 us
  local copies, waits for them, and re-layouts: 29.2 us -> 0.01 us
  matrix products: 16.4 us -> 0 us
  other arithmetic: 6.62 us -> 0 us
    pallas_call x0 -> x2, Pallas kernels: none -> 31.7 us  [the longest x1 16.7 us: _run_counts(): pl.pallas_call(_counts, name='counts', out_shape=[jax.ShapeDtypeStruct((b...]
    gather x2 -> x0, local copies, waits for them, and re-layouts: 27.9 us -> none  [the longest x1 24.3 us: local_run(): jnp.take(emit_loc.T, tokens.T.reshape(-1), axis=0, mode='clip')]
    dot_general x1 -> x0, matrix products: 16.4 us -> none  [local_run(): lax.dot_general(alphas.reshape(-1, bs), ws.reshape(-1, bs), (((0,), (0,))...]
    reduce_sum x5 -> x0, other arithmetic: 6.59 us -> none  [the longest x1 2.92 us: local_run(): tokens = jnp.sum(pick[:, :, None] * tokens_loc[None, :, :], axis=1)]
where the time goes in v3:
time: 394 us
  Pallas kernels  392 us (99%)
    pallas_call x1, Pallas kernels, _run_recursion(): pl.pallas_call(functools.partial(_recursion, caps), name=f'recursion{iden...  360 us
    pallas_call x1, Pallas kernels, _run_counts(): pl.pallas_call(_counts, name='counts', out_shape=[jax.ShapeDtypeStruct((b...  16.7 us
    pallas_call x1, Pallas kernels, _run_prepare(): pl.pallas_call(functools.partial(_prepare, caps), name='prepare', out_sha...  15 us

profile of v3, /device:TPU:81, one launch (start us, length us, event | category | flops | bytes accessed | tf_op | source)
XLA Modules:
  0.0 393.7 jit_solution(15315056659935158532)
XLA Ops:
  0.6 0.0 copy-start
  0.6 15.0 %prepare.1 = (bf16[8,128,2048]{2,1,0:T(8,128)(2,1)}, s32[128,128]{1,0:T(8,128)S(1)}, s32[8,128]{1,0:T(8,128)S(1)}, f32[8,128]{1,0:T(8,128)S(1)}, s32[1]{0:T(128)}) custom-call(s32[8,128]{1,0:T(8,128)} %bitcast.15, s32[1,128]{1,0:T(1,128)} %bitcast.16, bf16[1250,8,2048]{2,1,0:T(8,128)(2,1)} %bitcast.12), custom_call_target="tpu_custom_call" | custom-call | tf_op jit(solution)/shard_map/prepare/pallas_call | solution.py:532
  16.3 0.0 copy-done
  16.3 377.4 %conditional.1 = (f32[2048,2048]{1,0:T(8,128)}, f32[128,2048]{1,0:T(8,128)}, f32[128]{0:T(128)}) conditional(s32[]{:T(128)} %bitcast.10, (f32[2048]{0:T(1024)S(1)}, bf16[16384,2048]{1,0:T(8,128)(2,1)}, bf16[8,128,2048]{2,1,0:T(8,128)(2,1)}, s32[128,128]{1,0:T(8,128)S(1)}, s32[8,128]{1,0:T(8,128)S(1)}, /*index=5*/f32[8,128]{1,0:T(8,128)S(1)}) %tuple.22, ...), branch_computations={%region_0.0_spmd, %region_1.0_spmd} | conditional | flops 2 | bytes 44 | solution.py:636
  16.6 360.5 %recursion0.1 = (bf16[584,2048]{1,0:T(8,128)(2,1)}, bf16[584,2048]{1,0:T(8,128)(2,1)}, f32[128,2048]{1,0:T(8,128)}, f32[8,128]{1,0:T(8,128)}) custom-call(bf16[16384,2048]{1,0:T(8,128)(2,1)} %get-tuple-element.44.a_hbm.diag_ref, bf16[8,128,2048]{2,1,0:T(8,128)(2,1)} %get-tuple-element.45.em_hbm, f32[1,2048]{1,0:T(1,128)S(1)} %bitcast.14, ...), custom_call_target="tpu_custom_call" | custom-call | tf_op jit(solution)/shard_map/cond/branch_1_fun/recursion0/pallas_call | solution.py:428
  377.1 16.7 %counts.3 = (f32[2048,2048]{1,0:T(8,128)}, f32[128,2048]{1,0:T(8,128)}, f32[1,128]{1,0:T(1,128)}) custom-call(s32[1]{0:T(128)} %bitcast.3.block_ref, bf16[584,2048]{1,0:T(8,128)(2,1)} %get-tuple-element.49.alpha_ref, bf16[584,2048]{1,0:T(8,128)(2,1)} %get-tuple-element.50.w_ref, bf16[16384,2048]{1,0:T(8,128)(2,1)} %get-tuple-element.44.a_hbm.diag_ref, ...), custom_call_target="tpu_custom_call" | custom-call | tf_op jit(solution)/shard_map/cond/branch_1_fun/counts/pallas_call | solution.py:586
Async XLA Ops:
  0.6 15.7 %copy-start = (f32[2048]{0:T(1024)S(1)}, f32[2048]{0:T(1024)}, u32[]{:S(2)}) copy-start(f32[2048]{0:T(1024)} %param.9) | copy-start | bytes 24580
